TPU v7x, 32 devices: a whole 2x2x4 slice. The times are simulated.
32 devices in a mesh: dp: 4 (over y, x), ctx: 8 (over z, core).
Axes of the slice: x: 2, y: 2, z: 4, core: 2. Of those that a mesh axis runs over, the one named last changes fastest.
Arguments:
- query_rows: bfloat16 [4096, 2048], P(('dp', 'ctx')), may hold values from -64 to 64
- key_rows: bfloat16 [4096, 2048], P(('dp', 'ctx')), may hold values from -64 to 64
- value_rows: bfloat16 [4096, 2048], P(('dp', 'ctx')), may hold values from -6 to 6
- cotangent: bfloat16 [4096, 2048], P(('dp', 'ctx')), may hold values from -6 to 6
- query_gain: float32 [2048], replicated, may hold values from 0.5 to 5.5
- key_gain: float32 [2048], replicated, may hold values from 0.5 to 5.5
- positions: int32 [4096], P(('dp', 'ctx')), may hold values from 0 to 511, as said below
- span_start: int32 [8, 2], P('dp'), may hold values from 0 to 384, as said below
- span_length: int32 [8, 2], P('dp'), may hold values from 64 to 128
Outputs:
- output: bfloat16 [4096, 2048], P(('dp', 'ctx'))
- query_grad: bfloat16 [4096, 2048], P(('dp', 'ctx'))
- key_grad: bfloat16 [4096, 2048], P(('dp', 'ctx'))
- value_grad: bfloat16 [4096, 2048], P(('dp', 'ctx'))
- gain_grads: float32 [2, 2048], replicated
Inputs may be any that keep to these rules, and one draw needn't show every extreme that they name: Within each sequence every position 0 to 511 appears once; each block's rows are two runs of 64 consecutive positions, each run in increasing order. `span_start`: the first span of a sequence starts at 128 or earlier, the second at 256 or later; spans don't intersect and end inside the sequence.
All inputs are finite; a program needn't handle non-finite values.
Results may differ from a plain program's by a relative error of at most 0.035.
The roundings to bfloat16 on the way count: a program that leaves them out, or rounds other values in their place, can miss the bound.
Values may be sent and summed in bfloat16 or wider, within the bound.
A program may use at most 128 MiB of HBM per device.

v0:
```python
import functools

import jax
import jax.numpy as jnp
from jax import lax
from jax.experimental import pallas as pl
from jax.experimental.pallas import tpu as pltpu
from jax.sharding import PartitionSpec as P

HEAD = 128
SEQS_CTX = 2

epsilon = 1e-05
masked_score = -1e30
MESH = pl.DeviceIdType.MESH


def flip(index, distance, count):
    result = index
    bit = 1
    while bit < count:
        if distance & bit:
            result = result + bit - 2 * bit * ((index // bit) % 2)
        bit *= 2
    return result


def unit_of(raw):
    values = raw.astype(jnp.float32)
    inverse = lax.rsqrt(jnp.mean(values * values, axis=-1, keepdims=True) + epsilon)
    return values * inverse, inverse


def norm_backward(grad_normed, unit, inverse, gain):
    grad_unit = grad_normed * gain
    projected = jnp.mean(grad_unit * unit, axis=-1, keepdims=True)
    grad_raw = inverse * (grad_unit - unit * projected)
    return grad_raw.astype(jnp.bfloat16), jnp.sum(grad_normed * unit, axis=0, keepdims=True)


def dot(left, right, left_axis, right_axis):
    return lax.dot_general(
        left,
        right,
        (((left_axis,), (right_axis,)), ((), ())),
        preferred_element_type=jnp.float32,
    )


def kernel(
    members,
    dp_count,
    per_device,
    rows,
    query_in,
    key_in,
    value_in,
    cotangent_in,
    query_gain_in,
    key_gain_in,
    positions,
    span_start_in,
    span_length_in,
    out_ref,
    query_grad_ref,
    key_grad_ref,
    value_grad_ref,
    gain_ref,
    query_gain,
    key_gain,
    span_start,
    span_length,
    small_sem,
    in_buf,
    out_buf,
    bias,
    key_normed,
    key_total,
    value_total,
    places,
    gain_part,
    plane_buf,
    group_buf,
    in_send,
    in_recv,
    back_send,
    back_recv,
    place_send,
    place_recv,
    plane_send,
    plane_recv,
    group_send,
    group_recv,
):
    dp = lax.axis_index("dp")
    ctx = lax.axis_index("ctx")
    me = ctx // SEQS_CTX
    core = ctx % SEQS_CTX
    tokens = members * rows
    plane = dp_count * SEQS_CTX
    own = dp * SEQS_CTX + core
    sources = (query_in, key_in, value_in, cotangent_in)
    results = (out_ref, query_grad_ref, key_grad_ref, value_grad_ref)
    distances = range(members - 1, 0, -1)
    scale = HEAD ** (-0.5)

    def row_slice(member):
        return pl.ds(pl.multiple_of(member * rows, rows), rows)

    def head_slice(member, head):
        return pl.ds(pl.multiple_of((member * per_device + head) * HEAD, HEAD), HEAD)

    def member_device(distance):
        return (dp, flip(me, distance, members) * SEQS_CTX + core)

    def plane_device(step):
        other = (own + step) % plane
        return (other // SEQS_CTX, me * SEQS_CTX + other % SEQS_CTX)

    def copy_in(head, tensor, distance):
        if distance == 0:
            return pltpu.make_async_copy(
                sources[tensor].at[:, head_slice(me, head)],
                in_buf.at[head, tensor, row_slice(me), :],
                in_recv.at[head, tensor, 0],
            )
        return pltpu.make_async_remote_copy(
            src_ref=sources[tensor].at[:, head_slice(flip(me, distance, members), head)],
            dst_ref=in_buf.at[head, tensor, row_slice(me), :],
            send_sem=in_send.at[head, tensor, distance],
            recv_sem=in_recv.at[head, tensor, distance],
            device_id=member_device(distance),
            device_id_type=MESH,
        )

    def copy_back(head, tensor, distance):
        if distance == 0:
            return pltpu.make_async_copy(
                out_buf.at[head, tensor, row_slice(me), :],
                results[tensor].at[:, head_slice(me, head)],
                back_recv.at[head, tensor, 0],
            )
        return pltpu.make_async_remote_copy(
            src_ref=out_buf.at[head, tensor, row_slice(flip(me, distance, members)), :],
            dst_ref=results[tensor].at[:, head_slice(me, head)],
            send_sem=back_send.at[head, tensor, distance],
            recv_sem=back_recv.at[head, tensor, distance],
            device_id=member_device(distance),
            device_id_type=MESH,
        )

    def copy_places(distance):
        return pltpu.make_async_remote_copy(
            src_ref=positions,
            dst_ref=places.at[me],
            send_sem=place_send.at[distance],
            recv_sem=place_recv.at[distance],
            device_id=member_device(distance),
            device_id_type=MESH,
        )

    def copy_plane(step):
        return pltpu.make_async_remote_copy(
            src_ref=gain_part,
            dst_ref=plane_buf.at[own],
            send_sem=plane_send.at[step],
            recv_sem=plane_recv.at[step],
            device_id=plane_device(step),
            device_id_type=MESH,
        )

    def copy_group(distance):
        return pltpu.make_async_remote_copy(
            src_ref=gain_part,
            dst_ref=group_buf.at[me],
            send_sem=group_send.at[distance],
            recv_sem=group_recv.at[distance],
            device_id=member_device(distance),
            device_id_type=MESH,
        )

    barrier = pltpu.get_barrier_semaphore()
    for distance in distances:
        pl.semaphore_signal(barrier, 1, device_id=member_device(distance), device_id_type=MESH)
    for step in range(1, plane):
        pl.semaphore_signal(barrier, 1, device_id=plane_device(step), device_id_type=MESH)

    def start_own(head, carry):
        for tensor in range(4):
            copy_in(head, tensor, 0).start()
        return carry

    small_copies = [
        pltpu.make_async_copy(source, target, small_sem.at[index])
        for index, (source, target) in enumerate(
            (
                (positions, places.at[me]),
                (span_start_in, span_start),
                (span_length_in, span_length),
                (query_gain_in, query_gain),
                (key_gain_in, key_gain),
            )
        )
    ]
    for copy in small_copies:
        copy.start()
    lax.fori_loop(0, per_device, start_own, 0)
    pl.semaphore_wait(barrier, members - 1 + plane - 1)

    for distance in distances:
        copy_places(distance).start()

    def start_heads(head, carry):
        for distance in distances:
            for tensor in range(4):
                copy_in(head, tensor, distance).start()
        return carry

    lax.fori_loop(0, per_device, start_heads, 0)

    for copy in small_copies:
        copy.wait()
    for distance in distances:
        copy_places(distance).wait_recv()

    starts = [span_start[core, span] for span in range(span_start.shape[1])]
    ends = [
        starts[span] + span_length[core, span] for span in range(span_start.shape[1])
    ]

    def labels_of(place):
        label = jnp.zeros_like(place)
        for span in range(len(starts)):
            inside = (place >= starts[span]) & (place < ends[span])
            label = label + jnp.where(inside, span + 1, 0)
        return label

    def fill_bias(member, carry):
        row_places = jnp.transpose(jnp.broadcast_to(places[member], (rows, rows)))
        row_labels = labels_of(row_places)
        for other in range(members):
            key_places = jnp.broadcast_to(places[other], (rows, rows))
            key_labels = labels_of(key_places)
            allowed = (key_places <= row_places) | (
                (row_labels == key_labels) & (row_labels > 0)
            )
            bias[row_slice(member), other * rows : (other + 1) * rows] = jnp.where(
                allowed, 0.0, masked_score
            )
        return carry

    lax.fori_loop(0, members, fill_bias, 0)

    block = min(tokens, 256)

    def one_head(head, carry):
        for tensor in range(4):
            copy_in(head, tensor, 0).wait()
            for distance in distances:
                copy_in(head, tensor, distance).wait_recv()
        gain_q = query_gain[pl.ds(me * per_device + head, 1), :]
        gain_k = key_gain[pl.ds(me * per_device + head, 1), :]
        key_unit, key_inverse = unit_of(in_buf[head, 1])
        key_normed[...] = (key_unit * gain_k).astype(jnp.bfloat16)
        key_total[...] = jnp.zeros_like(key_total)
        value_total[...] = jnp.zeros_like(value_total)

        def one_block(index, query_part):
            here = pl.ds(pl.multiple_of(index * block, block), block)
            unit, inverse = unit_of(in_buf[head, 0, here, :])
            normed = (unit * gain_q).astype(jnp.bfloat16)
            values = in_buf[head, 2]
            grads = in_buf[head, 3, here, :]
            scores = dot(normed, key_normed[...], 1, 1) * scale + bias[here, :]
            row_max = jnp.max(scores, axis=-1, keepdims=True)
            powers = jnp.exp(scores - row_max)
            probs = powers * (1.0 / jnp.sum(powers, axis=-1, keepdims=True))
            weights = probs.astype(jnp.bfloat16)
            output = dot(weights, values, 1, 0).astype(jnp.bfloat16)
            out_buf[head, 0, here, :] = output
            delta = jnp.sum(
                output.astype(jnp.float32) * grads.astype(jnp.float32), axis=-1, keepdims=True
            )
            value_total[...] += dot(weights, grads, 0, 0)
            prob_grads = dot(grads, values, 1, 1)
            score_grads = (probs * (prob_grads - delta)).astype(jnp.bfloat16)
            grad_query = dot(score_grads, key_normed[...], 1, 0) * scale
            key_total[...] += dot(score_grads, normed, 0, 0)
            raw_grad, part = norm_backward(grad_query, unit, inverse, gain_q)
            out_buf[head, 1, here, :] = raw_grad
            return query_part + part

        query_part = jnp.zeros((1, HEAD), jnp.float32)
        if tokens // block <= 2:
            for index in range(tokens // block):
                query_part = one_block(index, query_part)
        else:
            query_part = lax.fori_loop(0, tokens // block, one_block, query_part)
        raw_grad, key_part = norm_backward(key_total[...] * scale, key_unit, key_inverse, gain_k)
        out_buf[head, 2] = raw_grad
        out_buf[head, 3] = value_total[...].astype(jnp.bfloat16)
        gain_part[pl.ds(head, 1), :] = query_part
        gain_part[pl.ds(per_device + head, 1), :] = key_part
        for distance in distances:
            for tensor in range(4):
                copy_back(head, tensor, distance).start()
        for tensor in range(4):
            copy_back(head, tensor, 0).start()
        return carry

    lax.fori_loop(0, per_device, one_head, 0)

    for step in range(1, plane):
        copy_plane(step).start()
    plane_buf[own] = gain_part[...]
    for step in range(1, plane):
        copy_plane(step).wait_recv()
    for step in range(1, plane):
        copy_plane(step).wait_send()
    total = plane_buf[0]
    for index in range(1, plane):
        total = total + plane_buf[index]
    gain_part[...] = total
    for distance in distances:
        copy_group(distance).start()
    group_buf[me] = total
    for distance in distances:
        copy_group(distance).wait_recv()
    for member in range(members):
        for head in range(per_device):
            at = (member * per_device + head) * HEAD
            gain_ref[0:1, at : at + HEAD] = group_buf[member, head : head + 1, :]
            gain_ref[1:2, at : at + HEAD] = group_buf[
                member, per_device + head : per_device + head + 1, :
            ]

    def finish(head, carry):
        for tensor in range(4):
            for distance in distances:
                copy_in(head, tensor, distance).wait_send()
                copy_back(head, tensor, distance).wait()
            copy_back(head, tensor, 0).wait()
        return carry

    lax.fori_loop(0, per_device, finish, 0)
    for distance in distances:
        copy_places(distance).wait_send()
        copy_group(distance).wait_send()


def place_results(*refs):
    count = len(refs) // 2
    copies = [
        pltpu.make_async_copy(refs[index], refs[count + index], refs[-1].at[index])
        for index in range(count)
    ]
    for copy in copies:
        copy.start()
    for copy in copies:
        copy.wait()


def body(
    members,
    dp_count,
    query_rows,
    key_rows,
    value_rows,
    cotangent,
    query_gain,
    key_gain,
    positions,
    span_start,
    span_length,
):
    rows, width = query_rows.shape
    heads = width // HEAD
    per_device = heads // members
    tokens = members * rows
    plane = dp_count * SEQS_CTX
    hbm = pl.BlockSpec(memory_space=pltpu.HBM)
    vmem = pl.BlockSpec(memory_space=pltpu.VMEM)
    wide = pltpu.VMEM((rows, width), jnp.bfloat16)
    dma = pltpu.SemaphoreType.DMA
    held = pl.pallas_call(
        functools.partial(kernel, members, dp_count, per_device, rows),
        out_shape=(wide, wide, wide, wide, pltpu.VMEM((2, width), jnp.float32)),
        in_specs=[hbm] * 9,
        out_specs=(vmem, vmem, vmem, vmem, vmem),
        scratch_shapes=[
            pltpu.VMEM((heads, HEAD), jnp.float32),
            pltpu.VMEM((heads, HEAD), jnp.float32),
            pltpu.SMEM(span_start.shape, jnp.int32),
            pltpu.SMEM(span_length.shape, jnp.int32),
            dma((5,)),
            pltpu.VMEM((per_device, 4, tokens, HEAD), jnp.bfloat16),
            pltpu.VMEM((per_device, 4, tokens, HEAD), jnp.bfloat16),
            pltpu.VMEM((tokens, tokens), jnp.float32),
            pltpu.VMEM((tokens, HEAD), jnp.bfloat16),
            pltpu.VMEM((tokens, HEAD), jnp.float32),
            pltpu.VMEM((tokens, HEAD), jnp.float32),
            pltpu.VMEM((members, 1, rows), jnp.int32),
            pltpu.VMEM((2 * per_device, HEAD), jnp.float32),
            pltpu.VMEM((plane, 2 * per_device, HEAD), jnp.float32),
            pltpu.VMEM((members, 2 * per_device, HEAD), jnp.float32),
            dma((per_device, 4, members)),
            dma((per_device, 4, members)),
            dma((per_device, 4, members)),
            dma((per_device, 4, members)),
            dma((members,)),
            dma((members,)),
            dma((plane,)),
            dma((plane,)),
            dma((members,)),
            dma((members,)),
        ],
        compiler_params=pltpu.CompilerParams(
            collective_id=0, has_side_effects=True, vmem_limit_bytes=123 * 512 * 1024
        ),
    )(
        query_rows,
        key_rows,
        value_rows,
        cotangent,
        query_gain.reshape(heads, HEAD),
        key_gain.reshape(heads, HEAD),
        positions.reshape(1, rows),
        span_start,
        span_length,
    )
    return pl.pallas_call(
        place_results,
        out_shape=tuple(jax.ShapeDtypeStruct(array.shape, array.dtype) for array in held),
        in_specs=[pl.BlockSpec(memory_space=pl.ANY)] * 5,
        out_specs=(pl.BlockSpec(memory_space=pltpu.HBM),) * 5,
        scratch_shapes=[dma((5,))],
        compiler_params=pltpu.CompilerParams(vmem_limit_bytes=1024 * 1024),
    )(*held)


def solution(mesh):
    row_spec = P(("dp", "ctx"), None)
    in_specs = (
        row_spec,
        row_spec,
        row_spec,
        row_spec,
        P(),
        P(),
        P(("dp", "ctx")),
        P("dp", None),
        P("dp", None),
    )
    out_specs = (row_spec, row_spec, row_spec, row_spec, P())
    members = mesh.shape["ctx"] // SEQS_CTX
    return jax.shard_map(
        functools.partial(body, members, mesh.shape["dp"]),
        mesh=mesh,
        in_specs=in_specs,
        out_specs=out_specs,
        check_vma=False,
    )
```

profile of v0, /device:TPU:0, one launch (start us, length us, event | category | flops | bytes accessed | tf_op | source)
XLA Modules:
  0.0 103.0 jit_solution(4634180930204157321)
XLA Ops:
  0.6 101.0 %shard_map.128 = (bf16[128,2048]{1,0:T(8,128)(2,1)S(1)}, bf16[128,2048]{1,0:T(8,128)(2,1)S(1)}, bf16[128,2048]{1,0:T(8,128)(2,1)S(1)}, bf16[128,2048]{1,0:T(8,128)(2,1)S(1)}, f32[2,2048]{1,0:T(2,128)S(1)}) custom-call(bf16[128,2048]{1,0:T(8,128)(2,1)} %query_in.1, bf16[128,2048]{1,0:T(8,128)(2,1)} %key_in.1, bf16[128,2048]{1,0:T(8,128)(2,1)} %value_in.1, ...), custom_call_target="tpu_custom_call" | custom-call | tf_op jit(solution)/shard_map/pallas_call | solution.py:385
  101.6 1.4 %shard_map.129 = (bf16[128,2048]{1,0:T(8,128)(2,1)}, bf16[128,2048]{1,0:T(8,128)(2,1)}, bf16[128,2048]{1,0:T(8,128)(2,1)}, bf16[128,2048]{1,0:T(8,128)(2,1)}, f32[2,2048]{1,0:T(2,128)}) custom-call(bf16[128,2048]{1,0:T(8,128)(2,1)S(1)} %get-tuple-element.10.refs_0_, bf16[128,2048]{1,0:T(8,128)(2,1)S(1)} %get-tuple-element.11.refs_1_, ...), custom_call_target="tpu_custom_call" | custom-call | tf_op jit(solution)/shard_map/pallas_call | solution.py:431
where the time goes:
time: 103 us
  Pallas kernels  102 us (99%)
    pallas_call x1, Pallas kernels, body(): pl.pallas_call(functools.partial(kernel, members, dp_count, per_device, r...  101 us

commit v1 on v0

--- a/solution.py
+++ b/solution.py
@@ -101,7 +101,7 @@
     own = dp * SEQS_CTX + core
     sources = (query_in, key_in, value_in, cotangent_in)
     results = (out_ref, query_grad_ref, key_grad_ref, value_grad_ref)
-    distances = range(members - 1, 0, -1)
+    distances = range(1, members)
     scale = HEAD ** (-0.5)
 
     def row_slice(member):

time: 103 us -> 103 us (level)
  no operation moved by 1% of the time
where the time goes in v1:
time: 103 us
  Pallas kernels  103 us (100%)
    pallas_call x1, Pallas kernels, body(): pl.pallas_call(functools.partial(kernel, members, dp_count, per_device, r...  101 us

profile of v1, /device:TPU:0, one launch (start us, length us, event | category | flops | bytes accessed | tf_op | source)
XLA Modules:
  0.0 103.2 jit_solution(4672643901141265826)
XLA Ops:
  0.6 101.2 %shard_map.128 = (bf16[128,2048]{1,0:T(8,128)(2,1)S(1)}, bf16[128,2048]{1,0:T(8,128)(2,1)S(1)}, bf16[128,2048]{1,0:T(8,128)(2,1)S(1)}, bf16[128,2048]{1,0:T(8,128)(2,1)S(1)}, f32[2,2048]{1,0:T(2,128)S(1)}) custom-call(bf16[128,2048]{1,0:T(8,128)(2,1)} %query_in.1, bf16[128,2048]{1,0:T(8,128)(2,1)} %key_in.1, bf16[128,2048]{1,0:T(8,128)(2,1)} %value_in.1, ...), custom_call_target="tpu_custom_call" | custom-call | tf_op jit(solution)/shard_map/pallas_call | solution.py:385
  101.8 1.4 %shard_map.129 = (bf16[128,2048]{1,0:T(8,128)(2,1)}, bf16[128,2048]{1,0:T(8,128)(2,1)}, bf16[128,2048]{1,0:T(8,128)(2,1)}, bf16[128,2048]{1,0:T(8,128)(2,1)}, f32[2,2048]{1,0:T(2,128)}) custom-call(bf16[128,2048]{1,0:T(8,128)(2,1)S(1)} %get-tuple-element.10.refs_0_, bf16[128,2048]{1,0:T(8,128)(2,1)S(1)} %get-tuple-element.11.refs_1_, ...), custom_call_target="tpu_custom_call" | custom-call | tf_op jit(solution)/shard_map/pallas_call | solution.py:431

commit v2 on v1

--- a/solution.py
+++ b/solution.py
@@ -9,6 +9,7 @@
 
 HEAD = 128
 SEQS_CTX = 2
+EARLY = 2
 
 epsilon = 1e-05
 masked_score = -1e30
@@ -81,6 +82,7 @@
     gain_part,
     plane_buf,
     group_buf,
+    ready,
     in_send,
     in_recv,
     back_send,
@@ -101,8 +103,22 @@
     own = dp * SEQS_CTX + core
     sources = (query_in, key_in, value_in, cotangent_in)
     results = (out_ref, query_grad_ref, key_grad_ref, value_grad_ref)
-    distances = range(1, members)
     scale = HEAD ** (-0.5)
+    half = members // 2
+    upper = me // half
+
+    def mirror(index):
+        return index + upper * (members - 1 - 2 * index)
+
+    spot = mirror(me)
+    middle = (spot + 1) // half
+    inner = mirror(spot + 1)
+    outer = mirror(spot - 1)
+    others = [mirror(members - 1 - step) for step in range(half - 1)]
+    if half > 1:
+        others.append(mirror(half + middle * ((spot + 1) % half - half)))
+    others += [mirror((spot + step) % half) for step in range(2, half)]
+    targets = others + [inner]
 
     def row_slice(member):
         return pl.ds(pl.multiple_of(member * rows, rows), rows)
@@ -110,84 +126,98 @@
     def head_slice(member, head):
         return pl.ds(pl.multiple_of((member * per_device + head) * HEAD, HEAD), HEAD)
 
-    def member_device(distance):
-        return (dp, flip(me, distance, members) * SEQS_CTX + core)
-
-    def plane_device(step):
-        other = (own + step) % plane
+    def device_of(member):
+        return (dp, member * SEQS_CTX + core)
+
+    def plane_device(bit):
+        other = flip(own, bit, plane)
         return (other // SEQS_CTX, me * SEQS_CTX + other % SEQS_CTX)
 
-    def copy_in(head, tensor, distance):
-        if distance == 0:
-            return pltpu.make_async_copy(
-                sources[tensor].at[:, head_slice(me, head)],
-                in_buf.at[head, tensor, row_slice(me), :],
-                in_recv.at[head, tensor, 0],
-            )
+    bits = [1 << index for index in range(plane.bit_length() - 1)]
+
+    def own_in(head, tensor):
+        return pltpu.make_async_copy(
+            sources[tensor].at[:, head_slice(me, head)],
+            in_buf.at[head, tensor, row_slice(me), :],
+            in_recv.at[head, tensor, me],
+        )
+
+    def copy_in(head, tensor, target, source=me):
         return pltpu.make_async_remote_copy(
-            src_ref=sources[tensor].at[:, head_slice(flip(me, distance, members), head)],
-            dst_ref=in_buf.at[head, tensor, row_slice(me), :],
-            send_sem=in_send.at[head, tensor, distance],
-            recv_sem=in_recv.at[head, tensor, distance],
-            device_id=member_device(distance),
+            src_ref=sources[tensor].at[:, head_slice(target, head)],
+            dst_ref=in_buf.at[head, tensor, row_slice(source), :],
+            send_sem=in_send.at[head, tensor, target],
+            recv_sem=in_recv.at[head, tensor, source],
+            device_id=device_of(target),
             device_id_type=MESH,
         )
 
-    def copy_back(head, tensor, distance):
-        if distance == 0:
-            return pltpu.make_async_copy(
-                out_buf.at[head, tensor, row_slice(me), :],
-                results[tensor].at[:, head_slice(me, head)],
-                back_recv.at[head, tensor, 0],
-            )
+    def own_back(head, tensor):
+        return pltpu.make_async_copy(
+            out_buf.at[head, tensor, row_slice(me), :],
+            results[tensor].at[:, head_slice(me, head)],
+            back_recv.at[head, tensor, me],
+        )
+
+    def copy_back(head, tensor, target, source=me):
         return pltpu.make_async_remote_copy(
-            src_ref=out_buf.at[head, tensor, row_slice(flip(me, distance, members)), :],
-            dst_ref=results[tensor].at[:, head_slice(me, head)],
-            send_sem=back_send.at[head, tensor, distance],
-            recv_sem=back_recv.at[head, tensor, distance],
-            device_id=member_device(distance),
+            src_ref=out_buf.at[head, tensor, row_slice(target), :],
+            dst_ref=results[tensor].at[:, head_slice(source, head)],
+            send_sem=back_send.at[head, tensor, target],
+            recv_sem=back_recv.at[head, tensor, source],
+            device_id=device_of(target),
             device_id_type=MESH,
         )
 
-    def copy_places(distance):
+    def copy_places(target, source=me):
         return pltpu.make_async_remote_copy(
             src_ref=positions,
-            dst_ref=places.at[me],
-            send_sem=place_send.at[distance],
-            recv_sem=place_recv.at[distance],
-            device_id=member_device(distance),
+            dst_ref=places.at[source],
+            send_sem=place_send.at[target],
+            recv_sem=place_recv.at[source],
+            device_id=device_of(target),
             device_id_type=MESH,
         )
 
-    def copy_plane(step):
+    def copy_plane(index):
         return pltpu.make_async_remote_copy(
-            src_ref=gain_part,
-            dst_ref=plane_buf.at[own],
-            send_sem=plane_send.at[step],
-            recv_sem=plane_recv.at[step],
-            device_id=plane_device(step),
+            src_ref=gain_part.at[index],
+            dst_ref=plane_buf.at[index],
+            send_sem=plane_send.at[index],
+            recv_sem=plane_recv.at[index],
+            device_id=plane_device(bits[index]),
             device_id_type=MESH,
         )
 
-    def copy_group(distance):
+    def copy_group(target, source=me):
         return pltpu.make_async_remote_copy(
-            src_ref=gain_part,
-            dst_ref=group_buf.at[me],
-            send_sem=group_send.at[distance],
-            recv_sem=group_recv.at[distance],
-            device_id=member_device(distance),
+            src_ref=gain_part.at[len(bits)],
+            dst_ref=group_buf.at[source],
+            send_sem=group_send.at[target],
+            recv_sem=group_recv.at[source],
+            device_id=device_of(target),
             device_id_type=MESH,
         )
 
+    def signal(semaphore, device):
+        pl.semaphore_signal(semaphore, 1, device_id=device, device_id_type=MESH)
+
     barrier = pltpu.get_barrier_semaphore()
-    for distance in distances:
-        pl.semaphore_signal(barrier, 1, device_id=member_device(distance), device_id_type=MESH)
-    for step in range(1, plane):
-        pl.semaphore_signal(barrier, 1, device_id=plane_device(step), device_id_type=MESH)
+
+    @pl.when(middle == 1)
+    def _():
+        signal(barrier, device_of(inner))
+
+    @pl.when(spot > 0)
+    def _():
+        signal(barrier, device_of(outer))
+
+    for bit in bits:
+        signal(barrier, plane_device(bit))
 
     def start_own(head, carry):
         for tensor in range(4):
-            copy_in(head, tensor, 0).start()
+            own_in(head, tensor).start()
         return carry
 
     small_copies = [
@@ -205,23 +235,58 @@
     for copy in small_copies:
         copy.start()
     lax.fori_loop(0, per_device, start_own, 0)
-    pl.semaphore_wait(barrier, members - 1 + plane - 1)
-
-    for distance in distances:
-        copy_places(distance).start()
-
-    def start_heads(head, carry):
-        for distance in distances:
+    pl.semaphore_wait(barrier, len(bits) + 1)
+
+    early = min(EARLY, per_device)
+
+    def start_inner(head, carry):
+        for tensor in range(4):
+            copy_in(head, tensor, inner).start()
+        return carry
+
+    copy_places(inner).start()
+    lax.fori_loop(0, early, start_inner, 0)
+
+    @pl.when(spot > 0)
+    def _():
+        pl.semaphore_wait(ready.at[0], 1)
+
+    @pl.when(middle == 0)
+    def _():
+        signal(ready.at[0], device_of(inner))
+        pl.semaphore_wait(ready.at[2], 1)
+
+    @pl.when(middle == 1)
+    def _():
+        signal(ready.at[1], device_of(inner))
+        pl.semaphore_wait(ready.at[1], 1)
+
+    @pl.when(spot > 0)
+    def _():
+        signal(ready.at[2], device_of(outer))
+
+    for target in others:
+        copy_places(target).start()
+
+    def start_others(head, carry):
+        for target in others:
             for tensor in range(4):
-                copy_in(head, tensor, distance).start()
-        return carry
-
-    lax.fori_loop(0, per_device, start_heads, 0)
+                copy_in(head, tensor, target).start()
+        return carry
+
+    def start_all(head, carry):
+        for target in targets:
+            for tensor in range(4):
+                copy_in(head, tensor, target).start()
+        return carry
+
+    lax.fori_loop(0, early, start_others, 0)
+    lax.fori_loop(early, per_device, start_all, 0)
 
     for copy in small_copies:
         copy.wait()
-    for distance in distances:
-        copy_places(distance).wait_recv()
+    for source in targets:
+        copy_places(inner, source).wait_recv()
 
     starts = [span_start[core, span] for span in range(span_start.shape[1])]
     ends = [
@@ -255,9 +320,9 @@
 
     def one_head(head, carry):
         for tensor in range(4):
-            copy_in(head, tensor, 0).wait()
-            for distance in distances:
-                copy_in(head, tensor, distance).wait_recv()
+            own_in(head, tensor).wait()
+            for source in targets:
+                copy_in(head, tensor, inner, source).wait_recv()
         gain_q = query_gain[pl.ds(me * per_device + head, 1), :]
         gain_k = key_gain[pl.ds(me * per_device + head, 1), :]
         key_unit, key_inverse = unit_of(in_buf[head, 1])
@@ -299,33 +364,34 @@
         raw_grad, key_part = norm_backward(key_total[...] * scale, key_unit, key_inverse, gain_k)
         out_buf[head, 2] = raw_grad
         out_buf[head, 3] = value_total[...].astype(jnp.bfloat16)
-        gain_part[pl.ds(head, 1), :] = query_part
-        gain_part[pl.ds(per_device + head, 1), :] = key_part
-        for distance in distances:
+        gain_part[0, pl.ds(head, 1), :] = query_part
+        gain_part[0, pl.ds(per_device + head, 1), :] = key_part
+        for tensor in range(4):
+            own_back(head, tensor).start()
+
+        @pl.when(head < per_device - 1)
+        def _():
+            start_back(head)
+
+        return carry
+
+    def start_back(head):
+        for target in targets:
             for tensor in range(4):
-                copy_back(head, tensor, distance).start()
-        for tensor in range(4):
-            copy_back(head, tensor, 0).start()
-        return carry
+                copy_back(head, tensor, target).start()
 
     lax.fori_loop(0, per_device, one_head, 0)
 
-    for step in range(1, plane):
-        copy_plane(step).start()
-    plane_buf[own] = gain_part[...]
-    for step in range(1, plane):
-        copy_plane(step).wait_recv()
-    for step in range(1, plane):
-        copy_plane(step).wait_send()
-    total = plane_buf[0]
-    for index in range(1, plane):
-        total = total + plane_buf[index]
-    gain_part[...] = total
-    for distance in distances:
-        copy_group(distance).start()
-    group_buf[me] = total
-    for distance in distances:
-        copy_group(distance).wait_recv()
+    for index in range(len(bits)):
+        copy_plane(index).start()
+        copy_plane(index).wait_recv()
+        gain_part[index + 1] = gain_part[index] + plane_buf[index]
+    for target in targets:
+        copy_group(target).start()
+    group_buf[me] = gain_part[len(bits)]
+    start_back(per_device - 1)
+    for source in targets:
+        copy_group(inner, source).wait_recv()
     for member in range(members):
         for head in range(per_device):
             at = (member * per_device + head) * HEAD
@@ -334,18 +400,22 @@
                 member, per_device + head : per_device + head + 1, :
             ]
 
+    for index in range(len(bits)):
+        copy_plane(index).wait_send()
+
     def finish(head, carry):
         for tensor in range(4):
-            for distance in distances:
-                copy_in(head, tensor, distance).wait_send()
-                copy_back(head, tensor, distance).wait()
-            copy_back(head, tensor, 0).wait()
+            for member in targets:
+                copy_in(head, tensor, member).wait_send()
+                copy_back(head, tensor, member).wait_send()
+                copy_back(head, tensor, inner, member).wait_recv()
+            own_back(head, tensor).wait()
         return carry
 
     lax.fori_loop(0, per_device, finish, 0)
-    for distance in distances:
-        copy_places(distance).wait_send()
-        copy_group(distance).wait_send()
+    for target in targets:
+        copy_places(target).wait_send()
+        copy_group(target).wait_send()
 
 
 def place_results(*refs):
@@ -377,7 +447,7 @@
     heads = width // HEAD
     per_device = heads // members
     tokens = members * rows
-    plane = dp_count * SEQS_CTX
+    rounds = (dp_count * SEQS_CTX).bit_length() - 1
     hbm = pl.BlockSpec(memory_space=pltpu.HBM)
     vmem = pl.BlockSpec(memory_space=pltpu.VMEM)
     wide = pltpu.VMEM((rows, width), jnp.bfloat16)
@@ -400,17 +470,18 @@
             pltpu.VMEM((tokens, HEAD), jnp.float32),
             pltpu.VMEM((tokens, HEAD), jnp.float32),
             pltpu.VMEM((members, 1, rows), jnp.int32),
-            pltpu.VMEM((2 * per_device, HEAD), jnp.float32),
-            pltpu.VMEM((plane, 2 * per_device, HEAD), jnp.float32),
+            pltpu.VMEM((rounds + 1, 2 * per_device, HEAD), jnp.float32),
+            pltpu.VMEM((rounds, 2 * per_device, HEAD), jnp.float32),
             pltpu.VMEM((members, 2 * per_device, HEAD), jnp.float32),
+            pltpu.SemaphoreType.REGULAR((3,)),
             dma((per_device, 4, members)),
             dma((per_device, 4, members)),
             dma((per_device, 4, members)),
             dma((per_device, 4, members)),
             dma((members,)),
             dma((members,)),
-            dma((plane,)),
-            dma((plane,)),
+            dma((rounds,)),
+            dma((rounds,)),
             dma((members,)),
             dma((members,)),
         ],

time: 103 us -> 99.8 us (0.969)
  the two profiles are of different devices: /device:TPU:0 before, /device:TPU:14 now
where the time goes in v2:
time: 99.8 us; the launch traced here: 98.3 us
  Pallas kernels  97.6 us (98%)
    pallas_call x1, Pallas kernels, body(): pl.pallas_call(functools.partial(kernel, members, dp_count, per_device, r...  96.3 us

profile of v2, /device:TPU:14, one launch (start us, length us, event | category | flops | bytes accessed | tf_op | source)
XLA Modules:
  0.0 98.3 jit_solution(2459946638939241129)
XLA Ops:
  0.6 96.3 %shard_map.128 = (bf16[128,2048]{1,0:T(8,128)(2,1)S(1)}, bf16[128,2048]{1,0:T(8,128)(2,1)S(1)}, bf16[128,2048]{1,0:T(8,128)(2,1)S(1)}, bf16[128,2048]{1,0:T(8,128)(2,1)S(1)}, f32[2,2048]{1,0:T(2,128)S(1)}) custom-call(bf16[128,2048]{1,0:T(8,128)(2,1)} %query_in.1, bf16[128,2048]{1,0:T(8,128)(2,1)} %key_in.1, bf16[128,2048]{1,0:T(8,128)(2,1)} %value_in.1, ...), custom_call_target="tpu_custom_call" | custom-call | tf_op jit(solution)/shard_map/pallas_call | solution.py:455
  96.9 1.4 %shard_map.129 = (bf16[128,2048]{1,0:T(8,128)(2,1)}, bf16[128,2048]{1,0:T(8,128)(2,1)}, bf16[128,2048]{1,0:T(8,128)(2,1)}, bf16[128,2048]{1,0:T(8,128)(2,1)}, f32[2,2048]{1,0:T(2,128)}) custom-call(bf16[128,2048]{1,0:T(8,128)(2,1)S(1)} %get-tuple-element.10.refs_0_, bf16[128,2048]{1,0:T(8,128)(2,1)S(1)} %get-tuple-element.11.refs_1_, ...), custom_call_target="tpu_custom_call" | custom-call | tf_op jit(solution)/shard_map/pallas_call | solution.py:502

commit v3 on v2

--- a/solution.py
+++ b/solution.py
@@ -139,42 +139,35 @@
         return pltpu.make_async_copy(
             sources[tensor].at[:, head_slice(me, head)],
             in_buf.at[head, tensor, row_slice(me), :],
-            in_recv.at[head, tensor, me],
-        )
-
-    def copy_in(head, tensor, target, source=me):
+            in_recv.at[head],
+        )
+
+    def copy_in(head, tensor, target):
         return pltpu.make_async_remote_copy(
             src_ref=sources[tensor].at[:, head_slice(target, head)],
-            dst_ref=in_buf.at[head, tensor, row_slice(source), :],
-            send_sem=in_send.at[head, tensor, target],
-            recv_sem=in_recv.at[head, tensor, source],
+            dst_ref=in_buf.at[head, tensor, row_slice(me), :],
+            send_sem=in_send.at[0],
+            recv_sem=in_recv.at[head],
             device_id=device_of(target),
             device_id_type=MESH,
         )
 
-    def own_back(head, tensor):
-        return pltpu.make_async_copy(
-            out_buf.at[head, tensor, row_slice(me), :],
-            results[tensor].at[:, head_slice(me, head)],
-            back_recv.at[head, tensor, me],
-        )
-
-    def copy_back(head, tensor, target, source=me):
+    def copy_back(head, tensor, target):
         return pltpu.make_async_remote_copy(
             src_ref=out_buf.at[head, tensor, row_slice(target), :],
-            dst_ref=results[tensor].at[:, head_slice(source, head)],
-            send_sem=back_send.at[head, tensor, target],
-            recv_sem=back_recv.at[head, tensor, source],
+            dst_ref=results[tensor].at[:, head_slice(me, head)],
+            send_sem=back_send.at[0],
+            recv_sem=back_recv.at[0],
             device_id=device_of(target),
             device_id_type=MESH,
         )
 
-    def copy_places(target, source=me):
+    def copy_places(target):
         return pltpu.make_async_remote_copy(
             src_ref=positions,
-            dst_ref=places.at[source],
-            send_sem=place_send.at[target],
-            recv_sem=place_recv.at[source],
+            dst_ref=places.at[me],
+            send_sem=place_send.at[0],
+            recv_sem=place_recv.at[0],
             device_id=device_of(target),
             device_id_type=MESH,
         )
@@ -189,16 +182,32 @@
             device_id_type=MESH,
         )
 
-    def copy_group(target, source=me):
+    def copy_group(target):
         return pltpu.make_async_remote_copy(
             src_ref=gain_part.at[len(bits)],
-            dst_ref=group_buf.at[source],
-            send_sem=group_send.at[target],
-            recv_sem=group_recv.at[source],
+            dst_ref=group_buf.at[me],
+            send_sem=group_send.at[0],
+            recv_sem=group_recv.at[0],
             device_id=device_of(target),
             device_id_type=MESH,
         )
 
+    def waiter(part, send, receive):
+        return pltpu.make_async_remote_copy(
+            src_ref=part,
+            dst_ref=part,
+            send_sem=send.at[0],
+            recv_sem=receive,
+            device_id=device_of(inner),
+            device_id_type=MESH,
+        )
+
+    elsewhere = pl.ds(0, (members - 1) * rows)
+    all_in = waiter(in_buf.at[:, :, elsewhere, :], in_send, in_recv.at[0])
+    all_back = waiter(out_buf.at[:, :, elsewhere, :], back_send, back_recv.at[0])
+    all_places = waiter(places.at[pl.ds(0, members - 1)], place_send, place_recv.at[0])
+    all_group = waiter(group_buf.at[pl.ds(0, members - 1)], group_send, group_recv.at[0])
+
     def signal(semaphore, device):
         pl.semaphore_signal(semaphore, 1, device_id=device, device_id_type=MESH)
 
@@ -212,8 +221,10 @@
     def _():
         signal(barrier, device_of(outer))
 
-    for bit in bits:
-        signal(barrier, plane_device(bit))
+    @pl.when(spot == 0)
+    def _():
+        for bit in bits:
+            signal(barrier, plane_device(bit))
 
     def start_own(head, carry):
         for tensor in range(4):
@@ -235,7 +246,7 @@
     for copy in small_copies:
         copy.start()
     lax.fori_loop(0, per_device, start_own, 0)
-    pl.semaphore_wait(barrier, len(bits) + 1)
+    pl.semaphore_wait(barrier, 1 + (half - spot) // half * len(bits))
 
     early = min(EARLY, per_device)
 
@@ -264,6 +275,11 @@
     @pl.when(spot > 0)
     def _():
         signal(ready.at[2], device_of(outer))
+
+    @pl.when(spot == 0)
+    def _():
+        for bit in bits:
+            signal(ready.at[3], plane_device(bit))
 
     for target in others:
         copy_places(target).start()
@@ -285,8 +301,7 @@
 
     for copy in small_copies:
         copy.wait()
-    for source in targets:
-        copy_places(inner, source).wait_recv()
+    all_places.wait_recv()
 
     starts = [span_start[core, span] for span in range(span_start.shape[1])]
     ends = [
@@ -319,10 +334,7 @@
     block = min(tokens, 256)
 
     def one_head(head, carry):
-        for tensor in range(4):
-            own_in(head, tensor).wait()
-            for source in targets:
-                copy_in(head, tensor, inner, source).wait_recv()
+        waiter(in_buf.at[head], in_send, in_recv.at[head]).wait_recv()
         gain_q = query_gain[pl.ds(me * per_device + head, 1), :]
         gain_k = key_gain[pl.ds(me * per_device + head, 1), :]
         key_unit, key_inverse = unit_of(in_buf[head, 1])
@@ -367,7 +379,7 @@
         gain_part[0, pl.ds(head, 1), :] = query_part
         gain_part[0, pl.ds(per_device + head, 1), :] = key_part
         for tensor in range(4):
-            own_back(head, tensor).start()
+            results[tensor][:, head_slice(me, head)] = out_buf[head, tensor, row_slice(me), :]
 
         @pl.when(head < per_device - 1)
         def _():
@@ -375,12 +387,31 @@
 
         return carry
 
-    def start_back(head):
-        for target in targets:
+    def start_back_to(head, chosen):
+        for target in chosen:
             for tensor in range(4):
                 copy_back(head, tensor, target).start()
 
+    def start_back(head):
+        start_back_to(head, others)
+
+        @pl.when(head > 0)
+        def _():
+            start_back_to(head - 1, [inner])
+
     lax.fori_loop(0, per_device, one_head, 0)
+
+    @pl.when(spot == 0)
+    def _():
+        pl.semaphore_wait(ready.at[3], len(bits))
+
+    @pl.when(spot > 0)
+    def _():
+        pl.semaphore_wait(ready.at[4], 1)
+
+    @pl.when(middle == 0)
+    def _():
+        signal(ready.at[4], device_of(inner))
 
     for index in range(len(bits)):
         copy_plane(index).start()
@@ -389,9 +420,11 @@
     for target in targets:
         copy_group(target).start()
     group_buf[me] = gain_part[len(bits)]
-    start_back(per_device - 1)
-    for source in targets:
-        copy_group(inner, source).wait_recv()
+    start_back_to(per_device - 1, others)
+    if per_device > 1:
+        start_back_to(per_device - 2, [inner])
+    start_back_to(per_device - 1, [inner])
+    all_group.wait_recv()
     for member in range(members):
         for head in range(per_device):
             at = (member * per_device + head) * HEAD
@@ -403,19 +436,11 @@
     for index in range(len(bits)):
         copy_plane(index).wait_send()
 
-    def finish(head, carry):
-        for tensor in range(4):
-            for member in targets:
-                copy_in(head, tensor, member).wait_send()
-                copy_back(head, tensor, member).wait_send()
-                copy_back(head, tensor, inner, member).wait_recv()
-            own_back(head, tensor).wait()
-        return carry
-
-    lax.fori_loop(0, per_device, finish, 0)
-    for target in targets:
-        copy_places(target).wait_send()
-        copy_group(target).wait_send()
+    all_in.wait_send()
+    all_places.wait_send()
+    all_group.wait_send()
+    all_back.wait_send()
+    all_back.wait_recv()
 
 
 def place_results(*refs):
@@ -473,17 +498,17 @@
             pltpu.VMEM((rounds + 1, 2 * per_device, HEAD), jnp.float32),
             pltpu.VMEM((rounds, 2 * per_device, HEAD), jnp.float32),
             pltpu.VMEM((members, 2 * per_device, HEAD), jnp.float32),
-            pltpu.SemaphoreType.REGULAR((3,)),
-            dma((per_device, 4, members)),
-            dma((per_device, 4, members)),
-            dma((per_device, 4, members)),
-            dma((per_device, 4, members)),
-            dma((members,)),
-            dma((members,)),
+            pltpu.SemaphoreType.REGULAR((5,)),
+            dma((1,)),
+            dma((per_device,)),
+            dma((1,)),
+            dma((1,)),
+            dma((1,)),
+            dma((1,)),
             dma((rounds,)),
             dma((rounds,)),
-            dma((members,)),
-            dma((members,)),
+            dma((1,)),
+            dma((1,)),
         ],
         compiler_params=pltpu.CompilerParams(
             collective_id=0, has_side_effects=True, vmem_limit_bytes=123 * 512 * 1024

time: 99.8 us -> 96.5 us (0.967)
  Pallas kernels: 97.6 us -> 94.8 us
    pallas_call x1, Pallas kernels: 96.3 us -> 93.4 us  [body(): pl.pallas_call(functools.partial(kernel, members, dp_count, per_device, r...]
where the time goes in v3:
time: 96.5 us; the launch traced here: 95.4 us
  Pallas kernels  94.8 us (98%)
    pallas_call x1, Pallas kernels, body(): pl.pallas_call(functools.partial(kernel, members, dp_count, per_device, r...  93.4 us

profile of v3, /device:TPU:14, one launch (start us, length us, event | category | flops | bytes accessed | tf_op | source)
XLA Modules:
  0.0 95.4 jit_solution(7223001367381446927)
XLA Ops:
  0.6 93.4 %shard_map.128 = (bf16[128,2048]{1,0:T(8,128)(2,1)S(1)}, bf16[128,2048]{1,0:T(8,128)(2,1)S(1)}, bf16[128,2048]{1,0:T(8,128)(2,1)S(1)}, bf16[128,2048]{1,0:T(8,128)(2,1)S(1)}, f32[2,2048]{1,0:T(2,128)S(1)}) custom-call(bf16[128,2048]{1,0:T(8,128)(2,1)} %query_in.1, bf16[128,2048]{1,0:T(8,128)(2,1)} %key_in.1, bf16[128,2048]{1,0:T(8,128)(2,1)} %value_in.1, ...), custom_call_target="tpu_custom_call" | custom-call | tf_op jit(solution)/shard_map/pallas_call | solution.py:480
  94.1 1.4 %shard_map.129 = (bf16[128,2048]{1,0:T(8,128)(2,1)}, bf16[128,2048]{1,0:T(8,128)(2,1)}, bf16[128,2048]{1,0:T(8,128)(2,1)}, bf16[128,2048]{1,0:T(8,128)(2,1)}, f32[2,2048]{1,0:T(2,128)}) custom-call(bf16[128,2048]{1,0:T(8,128)(2,1)S(1)} %get-tuple-element.10.refs_0_, bf16[128,2048]{1,0:T(8,128)(2,1)S(1)} %get-tuple-element.11.refs_1_, ...), custom_call_target="tpu_custom_call" | custom-call | tf_op jit(solution)/shard_map/pallas_call | solution.py:527

commit v4 on v3

--- a/solution.py
+++ b/solution.py
@@ -226,6 +226,18 @@
         for bit in bits:
             signal(barrier, plane_device(bit))
 
+    pl.semaphore_wait(barrier, 1 + (half - spot) // half * len(bits))
+
+    early = min(EARLY, per_device)
+
+    def start_inner(head, carry):
+        for tensor in range(4):
+            copy_in(head, tensor, inner).start()
+        return carry
+
+    copy_places(inner).start()
+    lax.fori_loop(0, early, start_inner, 0)
+
     def start_own(head, carry):
         for tensor in range(4):
             own_in(head, tensor).start()
@@ -246,17 +258,6 @@
     for copy in small_copies:
         copy.start()
     lax.fori_loop(0, per_device, start_own, 0)
-    pl.semaphore_wait(barrier, 1 + (half - spot) // half * len(bits))
-
-    early = min(EARLY, per_device)
-
-    def start_inner(head, carry):
-        for tensor in range(4):
-            copy_in(head, tensor, inner).start()
-        return carry
-
-    copy_places(inner).start()
-    lax.fori_loop(0, early, start_inner, 0)
 
     @pl.when(spot > 0)
     def _():
@@ -400,6 +401,7 @@
             start_back_to(head - 1, [inner])
 
     lax.fori_loop(0, per_device, one_head, 0)
+    start_back_to(per_device - 1, others)
 
     @pl.when(spot == 0)
     def _():
@@ -420,7 +422,6 @@
     for target in targets:
         copy_group(target).start()
     group_buf[me] = gain_part[len(bits)]
-    start_back_to(per_device - 1, others)
     if per_device > 1:
         start_back_to(per_device - 2, [inner])
     start_back_to(per_device - 1, [inner])

time: 96.5 us -> 95.6 us (level)
  no operation moved by 1% of the time
where the time goes in v4:
time: 95.6 us; the launch traced here: 95.5 us
  Pallas kernels  94.8 us (99%)
    pallas_call x1, Pallas kernels, body(): pl.pallas_call(functools.partial(kernel, members, dp_count, per_device, r...  93.5 us

profile of v4, /device:TPU:14, one launch (start us, length us, event | category | flops | bytes accessed | tf_op | source)
XLA Modules:
  0.0 95.5 jit_solution(6327242751623344203)
XLA Ops:
  0.6 93.5 %shard_map.128 = (bf16[128,2048]{1,0:T(8,128)(2,1)S(1)}, bf16[128,2048]{1,0:T(8,128)(2,1)S(1)}, bf16[128,2048]{1,0:T(8,128)(2,1)S(1)}, bf16[128,2048]{1,0:T(8,128)(2,1)S(1)}, f32[2,2048]{1,0:T(2,128)S(1)}) custom-call(bf16[128,2048]{1,0:T(8,128)(2,1)} %query_in.1, bf16[128,2048]{1,0:T(8,128)(2,1)} %key_in.1, bf16[128,2048]{1,0:T(8,128)(2,1)} %value_in.1, ...), custom_call_target="tpu_custom_call" | custom-call | tf_op jit(solution)/shard_map/pallas_call | solution.py:481
  94.1 1.4 %shard_map.129 = (bf16[128,2048]{1,0:T(8,128)(2,1)}, bf16[128,2048]{1,0:T(8,128)(2,1)}, bf16[128,2048]{1,0:T(8,128)(2,1)}, bf16[128,2048]{1,0:T(8,128)(2,1)}, f32[2,2048]{1,0:T(2,128)}) custom-call(bf16[128,2048]{1,0:T(8,128)(2,1)S(1)} %get-tuple-element.10.refs_0_, bf16[128,2048]{1,0:T(8,128)(2,1)S(1)} %get-tuple-element.11.refs_1_, ...), custom_call_target="tpu_custom_call" | custom-call | tf_op jit(solution)/shard_map/pallas_call | solution.py:528

commit v5 on v4

--- a/solution.py
+++ b/solution.py
@@ -10,6 +10,7 @@
 HEAD = 128
 SEQS_CTX = 2
 EARLY = 2
+RELAYED = 1
 
 epsilon = 1e-05
 masked_score = -1e30
@@ -82,6 +83,7 @@
     gain_part,
     plane_buf,
     group_buf,
+    relay_buf,
     ready,
     in_send,
     in_recv,
@@ -93,6 +95,10 @@
     plane_recv,
     group_send,
     group_recv,
+    share_send,
+    share_recv,
+    relay_send,
+    relay_recv,
 ):
     dp = lax.axis_index("dp")
     ctx = lax.axis_index("ctx")
@@ -159,6 +165,42 @@
             send_sem=back_send.at[0],
             recv_sem=back_recv.at[0],
             device_id=device_of(target),
+            device_id_type=MESH,
+        )
+
+    carried = range(4 - (RELAYED if per_device > 1 else 0), 4)
+    gives = middle * (1 - core)
+    carries = middle * core
+    first_of = lambda index: 1 - jnp.minimum(index, 1)
+    other_core = (dp, me * SEQS_CTX + 1 - core)
+
+    def copy_over(tensor):
+        return pltpu.make_async_remote_copy(
+            src_ref=out_buf.at[0, tensor, row_slice(inner), :],
+            dst_ref=relay_buf.at[tensor - carried[0]],
+            send_sem=back_send.at[0],
+            recv_sem=relay_recv.at[0],
+            device_id=other_core,
+            device_id_type=MESH,
+        )
+
+    def copy_carried(tensor):
+        return pltpu.make_async_remote_copy(
+            src_ref=relay_buf.at[tensor - carried[0]],
+            dst_ref=results[tensor].at[:, head_slice(me, 0)],
+            send_sem=relay_send.at[0],
+            recv_sem=back_recv.at[0],
+            device_id=(dp, inner * SEQS_CTX),
+            device_id_type=MESH,
+        )
+
+    def copy_share():
+        return pltpu.make_async_remote_copy(
+            src_ref=group_buf,
+            dst_ref=group_buf,
+            send_sem=share_send.at[0],
+            recv_sem=share_recv.at[0],
+            device_id=other_core,
             device_id_type=MESH,
         )
 
@@ -382,50 +424,83 @@
         for tensor in range(4):
             results[tensor][:, head_slice(me, head)] = out_buf[head, tensor, row_slice(me), :]
 
+        if len(carried) > 0:
+
+            @pl.when(gives * first_of(head) == 1)
+            def _():
+                for tensor in carried:
+                    copy_over(tensor).start()
+
+            @pl.when(carries * first_of(jnp.abs(head - 1)) == 1)
+            def _():
+                waiter(relay_buf, relay_send, relay_recv.at[0]).wait_recv()
+                for tensor in carried:
+                    copy_carried(tensor).start()
+
         @pl.when(head < per_device - 1)
         def _():
             start_back(head)
 
         return carry
 
-    def start_back_to(head, chosen):
+    def start_back_to(head, chosen, tensors=range(4)):
         for target in chosen:
-            for tensor in range(4):
+            for tensor in tensors:
                 copy_back(head, tensor, target).start()
+
+    def start_back_inner(head):
+        start_back_to(head, [inner], range(carried[0] if len(carried) > 0 else 4))
+        if len(carried) > 0:
+
+            @pl.when(gives * first_of(head) == 0)
+            def _():
+                start_back_to(head, [inner], carried)
 
     def start_back(head):
         start_back_to(head, others)
 
         @pl.when(head > 0)
         def _():
-            start_back_to(head - 1, [inner])
+            start_back_inner(head - 1)
+
+    @pl.when(spot == 0)
+    def _():
+        pl.semaphore_wait(ready.at[3], len(bits))
+
+    @pl.when(spot > 0)
+    def _():
+        pl.semaphore_wait(ready.at[4], 1)
+
+    @pl.when(middle == 0)
+    def _():
+        signal(ready.at[4], device_of(inner))
 
     lax.fori_loop(0, per_device, one_head, 0)
     start_back_to(per_device - 1, others)
-
-    @pl.when(spot == 0)
-    def _():
-        pl.semaphore_wait(ready.at[3], len(bits))
-
-    @pl.when(spot > 0)
-    def _():
-        pl.semaphore_wait(ready.at[4], 1)
-
-    @pl.when(middle == 0)
-    def _():
-        signal(ready.at[4], device_of(inner))
 
     for index in range(len(bits)):
         copy_plane(index).start()
         copy_plane(index).wait_recv()
         gain_part[index + 1] = gain_part[index] + plane_buf[index]
-    for target in targets:
-        copy_group(target).start()
-    group_buf[me] = gain_part[len(bits)]
+    @pl.when(core == 1)
+    def _():
+        group_buf[me] = gain_part[len(bits)]
+        for target in targets:
+            copy_group(target).start()
+
     if per_device > 1:
-        start_back_to(per_device - 2, [inner])
-    start_back_to(per_device - 1, [inner])
-    all_group.wait_recv()
+        start_back_inner(per_device - 2)
+    start_back_inner(per_device - 1)
+
+    @pl.when(core == 1)
+    def _():
+        all_group.wait_recv()
+        copy_share().start()
+
+    @pl.when(core == 0)
+    def _():
+        copy_share().wait_recv()
+
     for member in range(members):
         for head in range(per_device):
             at = (member * per_device + head) * HEAD
@@ -439,8 +514,19 @@
 
     all_in.wait_send()
     all_places.wait_send()
-    all_group.wait_send()
+
+    @pl.when(core == 1)
+    def _():
+        all_group.wait_send()
+        copy_share().wait_send()
+
     all_back.wait_send()
+    if len(carried) > 0:
+
+        @pl.when(carries == 1)
+        def _():
+            waiter(relay_buf, relay_send, relay_recv.at[0]).wait_send()
+
     all_back.wait_recv()
 
 
@@ -499,6 +585,7 @@
             pltpu.VMEM((rounds + 1, 2 * per_device, HEAD), jnp.float32),
             pltpu.VMEM((rounds, 2 * per_device, HEAD), jnp.float32),
             pltpu.VMEM((members, 2 * per_device, HEAD), jnp.float32),
+            pltpu.VMEM((max(RELAYED, 1), rows, HEAD), jnp.bfloat16),
             pltpu.SemaphoreType.REGULAR((5,)),
             dma((1,)),
             dma((per_device,)),
@@ -508,6 +595,10 @@
             dma((1,)),
             dma((rounds,)),
             dma((rounds,)),
+            dma((1,)),
+            dma((1,)),
+            dma((1,)),
+            dma((1,)),
             dma((1,)),
             dma((1,)),
         ],

time: 95.6 us -> 95.5 us (level)
  no operation moved by 1% of the time
where the time goes in v5:
time: 95.5 us; the launch traced here: 95.3 us
  Pallas kernels  94.7 us (99%)
    pallas_call x1, Pallas kernels, body(): pl.pallas_call(functools.partial(kernel, members, dp_count, per_device, r...  93.3 us

profile of v5, /device:TPU:14, one launch (start us, length us, event | category | flops | bytes accessed | tf_op | source)
XLA Modules:
  0.0 95.3 jit_solution(2046740749992490444)
XLA Ops:
  0.6 93.3 %shard_map.128 = (bf16[128,2048]{1,0:T(8,128)(2,1)S(1)}, bf16[128,2048]{1,0:T(8,128)(2,1)S(1)}, bf16[128,2048]{1,0:T(8,128)(2,1)S(1)}, bf16[128,2048]{1,0:T(8,128)(2,1)S(1)}, f32[2,2048]{1,0:T(2,128)S(1)}) custom-call(bf16[128,2048]{1,0:T(8,128)(2,1)} %query_in.1, bf16[128,2048]{1,0:T(8,128)(2,1)} %key_in.1, bf16[128,2048]{1,0:T(8,128)(2,1)} %value_in.1, ...), custom_call_target="tpu_custom_call" | custom-call | tf_op jit(solution)/shard_map/pallas_call | solution.py:567
  94.0 1.4 %shard_map.129 = (bf16[128,2048]{1,0:T(8,128)(2,1)}, bf16[128,2048]{1,0:T(8,128)(2,1)}, bf16[128,2048]{1,0:T(8,128)(2,1)}, bf16[128,2048]{1,0:T(8,128)(2,1)}, f32[2,2048]{1,0:T(2,128)}) custom-call(bf16[128,2048]{1,0:T(8,128)(2,1)S(1)} %get-tuple-element.10.refs_0_, bf16[128,2048]{1,0:T(8,128)(2,1)S(1)} %get-tuple-element.11.refs_1_, ...), custom_call_target="tpu_custom_call" | custom-call | tf_op jit(solution)/shard_map/pallas_call | solution.py:619

commit v6 on v4

--- a/solution.py
+++ b/solution.py
@@ -67,10 +67,8 @@
     key_grad_ref,
     value_grad_ref,
     gain_ref,
-    query_gain,
-    key_gain,
-    span_start,
-    span_length,
+    gains,
+    spans,
     small_sem,
     in_buf,
     out_buf,
@@ -93,6 +91,8 @@
     plane_recv,
     group_send,
     group_recv,
+    share_send,
+    share_recv,
 ):
     dp = lax.axis_index("dp")
     ctx = lax.axis_index("ctx")
@@ -162,6 +162,16 @@
             device_id_type=MESH,
         )
 
+    def copy_share():
+        return pltpu.make_async_remote_copy(
+            src_ref=group_buf,
+            dst_ref=group_buf,
+            send_sem=share_send.at[0],
+            recv_sem=share_recv.at[0],
+            device_id=(dp, me * SEQS_CTX + 1 - core),
+            device_id_type=MESH,
+        )
+
     def copy_places(target):
         return pltpu.make_async_remote_copy(
             src_ref=positions,
@@ -176,7 +186,7 @@
         return pltpu.make_async_remote_copy(
             src_ref=gain_part.at[index],
             dst_ref=plane_buf.at[index],
-            send_sem=plane_send.at[index],
+            send_sem=plane_send.at[0],
             recv_sem=plane_recv.at[index],
             device_id=plane_device(bits[index]),
             device_id_type=MESH,
@@ -244,16 +254,11 @@
         return carry
 
     small_copies = [
-        pltpu.make_async_copy(source, target, small_sem.at[index])
-        for index, (source, target) in enumerate(
-            (
-                (positions, places.at[me]),
-                (span_start_in, span_start),
-                (span_length_in, span_length),
-                (query_gain_in, query_gain),
-                (key_gain_in, key_gain),
-            )
-        )
+        pltpu.make_async_copy(positions, places.at[me], place_recv.at[0]),
+        pltpu.make_async_copy(span_start_in, spans.at[0], small_sem.at[0]),
+        pltpu.make_async_copy(span_length_in, spans.at[1], small_sem.at[0]),
+        pltpu.make_async_copy(query_gain_in, gains.at[0], small_sem.at[1]),
+        pltpu.make_async_copy(key_gain_in, gains.at[1], small_sem.at[1]),
     ]
     for copy in small_copies:
         copy.start()
@@ -266,7 +271,7 @@
     @pl.when(middle == 0)
     def _():
         signal(ready.at[0], device_of(inner))
-        pl.semaphore_wait(ready.at[2], 1)
+        pl.semaphore_wait(ready.at[1], 1)
 
     @pl.when(middle == 1)
     def _():
@@ -275,12 +280,12 @@
 
     @pl.when(spot > 0)
     def _():
-        signal(ready.at[2], device_of(outer))
+        signal(ready.at[1], device_of(outer))
 
     @pl.when(spot == 0)
     def _():
         for bit in bits:
-            signal(ready.at[3], plane_device(bit))
+            signal(ready.at[2], plane_device(bit))
 
     for target in others:
         copy_places(target).start()
@@ -300,13 +305,13 @@
     lax.fori_loop(0, early, start_others, 0)
     lax.fori_loop(early, per_device, start_all, 0)
 
-    for copy in small_copies:
-        copy.wait()
-    all_places.wait_recv()
-
-    starts = [span_start[core, span] for span in range(span_start.shape[1])]
+    pltpu.make_async_copy(spans, spans, small_sem.at[0]).wait()
+    pltpu.make_async_copy(gains, gains, small_sem.at[1]).wait()
+    waiter(places, place_send, place_recv.at[0]).wait_recv()
+
+    starts = [spans[0, core, span] for span in range(spans.shape[2])]
     ends = [
-        starts[span] + span_length[core, span] for span in range(span_start.shape[1])
+        starts[span] + spans[1, core, span] for span in range(spans.shape[2])
     ]
 
     def labels_of(place):
@@ -336,8 +341,8 @@
 
     def one_head(head, carry):
         waiter(in_buf.at[head], in_send, in_recv.at[head]).wait_recv()
-        gain_q = query_gain[pl.ds(me * per_device + head, 1), :]
-        gain_k = key_gain[pl.ds(me * per_device + head, 1), :]
+        gain_q = gains[0, pl.ds(me * per_device + head, 1), :]
+        gain_k = gains[1, pl.ds(me * per_device + head, 1), :]
         key_unit, key_inverse = unit_of(in_buf[head, 1])
         key_normed[...] = (key_unit * gain_k).astype(jnp.bfloat16)
         key_total[...] = jnp.zeros_like(key_total)
@@ -405,27 +410,39 @@
 
     @pl.when(spot == 0)
     def _():
-        pl.semaphore_wait(ready.at[3], len(bits))
+        pl.semaphore_wait(ready.at[2], len(bits))
 
     @pl.when(spot > 0)
     def _():
-        pl.semaphore_wait(ready.at[4], 1)
+        pl.semaphore_wait(ready.at[3], 1)
 
     @pl.when(middle == 0)
     def _():
-        signal(ready.at[4], device_of(inner))
+        signal(ready.at[3], device_of(inner))
 
     for index in range(len(bits)):
         copy_plane(index).start()
         copy_plane(index).wait_recv()
         gain_part[index + 1] = gain_part[index] + plane_buf[index]
-    for target in targets:
-        copy_group(target).start()
-    group_buf[me] = gain_part[len(bits)]
+    @pl.when(core == 1)
+    def _():
+        group_buf[me] = gain_part[len(bits)]
+        for target in targets:
+            copy_group(target).start()
+
     if per_device > 1:
         start_back_to(per_device - 2, [inner])
     start_back_to(per_device - 1, [inner])
-    all_group.wait_recv()
+
+    @pl.when(core == 1)
+    def _():
+        all_group.wait_recv()
+        copy_share().start()
+
+    @pl.when(core == 0)
+    def _():
+        copy_share().wait_recv()
+
     for member in range(members):
         for head in range(per_device):
             at = (member * per_device + head) * HEAD
@@ -434,12 +451,16 @@
                 member, per_device + head : per_device + head + 1, :
             ]
 
-    for index in range(len(bits)):
-        copy_plane(index).wait_send()
+    waiter(plane_buf, plane_send, plane_recv.at[0]).wait_send()
 
     all_in.wait_send()
     all_places.wait_send()
-    all_group.wait_send()
+
+    @pl.when(core == 1)
+    def _():
+        all_group.wait_send()
+        copy_share().wait_send()
+
     all_back.wait_send()
     all_back.wait_recv()
 
@@ -484,11 +505,9 @@
         in_specs=[hbm] * 9,
         out_specs=(vmem, vmem, vmem, vmem, vmem),
         scratch_shapes=[
-            pltpu.VMEM((heads, HEAD), jnp.float32),
-            pltpu.VMEM((heads, HEAD), jnp.float32),
-            pltpu.SMEM(span_start.shape, jnp.int32),
-            pltpu.SMEM(span_length.shape, jnp.int32),
-            dma((5,)),
+            pltpu.VMEM((2, heads, HEAD), jnp.float32),
+            pltpu.SMEM((2,) + span_start.shape, jnp.int32),
+            dma((2,)),
             pltpu.VMEM((per_device, 4, tokens, HEAD), jnp.bfloat16),
             pltpu.VMEM((per_device, 4, tokens, HEAD), jnp.bfloat16),
             pltpu.VMEM((tokens, tokens), jnp.float32),
@@ -499,15 +518,17 @@
             pltpu.VMEM((rounds + 1, 2 * per_device, HEAD), jnp.float32),
             pltpu.VMEM((rounds, 2 * per_device, HEAD), jnp.float32),
             pltpu.VMEM((members, 2 * per_device, HEAD), jnp.float32),
-            pltpu.SemaphoreType.REGULAR((5,)),
+            pltpu.SemaphoreType.REGULAR((4,)),
             dma((1,)),
             dma((per_device,)),
             dma((1,)),
             dma((1,)),
             dma((1,)),
             dma((1,)),
+            dma((1,)),
             dma((rounds,)),
-            dma((rounds,)),
+            dma((1,)),
+            dma((1,)),
             dma((1,)),
             dma((1,)),
         ],

time: 95.6 us -> 95.4 us (level)
  no operation moved by 1% of the time
where the time goes in v6:
time: 95.4 us; the launch traced here: 95.3 us
  Pallas kernels  94.6 us (99%)
    pallas_call x1, Pallas kernels, body(): pl.pallas_call(functools.partial(kernel, members, dp_count, per_device, r...  93.3 us

profile of v6, /device:TPU:14, one launch (start us, length us, event | category | flops | bytes accessed | tf_op | source)
XLA Modules:
  0.0 95.3 jit_solution(12800859999337359866)
XLA Ops:
  0.6 93.3 %shard_map.128 = (bf16[128,2048]{1,0:T(8,128)(2,1)S(1)}, bf16[128,2048]{1,0:T(8,128)(2,1)S(1)}, bf16[128,2048]{1,0:T(8,128)(2,1)S(1)}, bf16[128,2048]{1,0:T(8,128)(2,1)S(1)}, f32[2,2048]{1,0:T(2,128)S(1)}) custom-call(bf16[128,2048]{1,0:T(8,128)(2,1)} %query_in.1, bf16[128,2048]{1,0:T(8,128)(2,1)} %key_in.1, bf16[128,2048]{1,0:T(8,128)(2,1)} %value_in.1, ...), custom_call_target="tpu_custom_call" | custom-call | tf_op jit(solution)/shard_map/pallas_call | solution.py:502
  93.9 1.4 %shard_map.129 = (bf16[128,2048]{1,0:T(8,128)(2,1)}, bf16[128,2048]{1,0:T(8,128)(2,1)}, bf16[128,2048]{1,0:T(8,128)(2,1)}, bf16[128,2048]{1,0:T(8,128)(2,1)}, f32[2,2048]{1,0:T(2,128)}) custom-call(bf16[128,2048]{1,0:T(8,128)(2,1)S(1)} %get-tuple-element.10.refs_0_, bf16[128,2048]{1,0:T(8,128)(2,1)S(1)} %get-tuple-element.11.refs_1_, ...), custom_call_target="tpu_custom_call" | custom-call | tf_op jit(solution)/shard_map/pallas_call | solution.py:549

commit v7 on v6

--- a/solution.py
+++ b/solution.py
@@ -245,8 +245,8 @@
             copy_in(head, tensor, inner).start()
         return carry
 
+    lax.fori_loop(0, early, start_inner, 0)
     copy_places(inner).start()
-    lax.fori_loop(0, early, start_inner, 0)
 
     def start_own(head, carry):
         for tensor in range(4):

time: 95.4 us -> 95.4 us (level)
  no operation moved by 1% of the time
where the time goes in v7:
time: 95.4 us; the launch traced here: 95.3 us
  Pallas kernels  94.6 us (99%)
    pallas_call x1, Pallas kernels, body(): pl.pallas_call(functools.partial(kernel, members, dp_count, per_device, r...  93.3 us

profile of v7, /device:TPU:14, one launch (start us, length us, event | category | flops | bytes accessed | tf_op | source)
XLA Modules:
  0.0 95.3 jit_solution(11918288719395861282)
XLA Ops:
  0.6 93.3 %shard_map.128 = (bf16[128,2048]{1,0:T(8,128)(2,1)S(1)}, bf16[128,2048]{1,0:T(8,128)(2,1)S(1)}, bf16[128,2048]{1,0:T(8,128)(2,1)S(1)}, bf16[128,2048]{1,0:T(8,128)(2,1)S(1)}, f32[2,2048]{1,0:T(2,128)S(1)}) custom-call(bf16[128,2048]{1,0:T(8,128)(2,1)} %query_in.1, bf16[128,2048]{1,0:T(8,128)(2,1)} %key_in.1, bf16[128,2048]{1,0:T(8,128)(2,1)} %value_in.1, ...), custom_call_target="tpu_custom_call" | custom-call | tf_op jit(solution)/shard_map/pallas_call | solution.py:502
  93.9 1.4 %shard_map.129 = (bf16[128,2048]{1,0:T(8,128)(2,1)}, bf16[128,2048]{1,0:T(8,128)(2,1)}, bf16[128,2048]{1,0:T(8,128)(2,1)}, bf16[128,2048]{1,0:T(8,128)(2,1)}, f32[2,2048]{1,0:T(2,128)}) custom-call(bf16[128,2048]{1,0:T(8,128)(2,1)S(1)} %get-tuple-element.10.refs_0_, bf16[128,2048]{1,0:T(8,128)(2,1)S(1)} %get-tuple-element.11.refs_1_, ...), custom_call_target="tpu_custom_call" | custom-call | tf_op jit(solution)/shard_map/pallas_call | solution.py:549
